TPU v7x, 32 devices: a whole 2x2x4 slice. The times are simulated.
32 devices in a mesh: depth: 4 (over z), imgx: 4 (over y, core), imgy: 2 (over x).
Axes of the slice: x: 2, y: 2, z: 4, core: 2. Of those that a mesh axis runs over, the one named last changes fastest.
Arguments:
- emissivity: bfloat16 [32, 512, 256], P('depth', 'imgx', 'imgy'), may hold values from 0.099609375 to 10
- bin_index: int32 [32, 512, 256], P('depth', 'imgx', 'imgy'), may hold values from 0 to 127
- color_table: bfloat16 [4, 128], replicated, may hold values from 0.049804688 to 1
- brick_order: int32 [4], replicated, may hold values from 0 to 3, each once
Outputs:
- image: float32 [4, 512, 256], P(None, 'imgx', 'imgy')
Inputs may be any that keep to these rules, and one draw needn't show every extreme that they name: brick_order names every brick index once.
All inputs are finite; a program needn't handle non-finite values.
Results may differ from a plain program's by a relative error of at most 0.0003.
Values sent between devices are 32-bit elements; how exact they have to be, the bound alone decides.
No kernel may reach another device: no remote copies, remote signals or barrier semaphores. Data moves between devices by JAX's collectives and lax.ppermute only.
A program may use at most 64 MiB of HBM per device.

v0:
```python
import functools
import math

import jax
import jax.numpy as jnp
from jax import lax
from jax.experimental import pallas as pl
from jax.experimental.pallas import tpu as pltpu
from jax.sharding import PartitionSpec as P


LANES = 128
TABLE_STEPS = 4096.0
FIELD_BITS = 13
FIELD = 1 << FIELD_BITS
ROWS = 8
READY = (3,)
OUT_ORDER = ((1, 3, 0, 2), (3, 2, 1, 0), (2, 0, 3, 1))
BACK_ORDER = ((1, 2, 3, 0), (2, 3, 0, 1), (3, 0, 1, 2))
LANE_GATHER = lax.GatherDimensionNumbers(
    offset_dims=(),
    collapsed_slice_dims=(1,),
    start_index_map=(1,),
    operand_batching_dims=(0,),
    start_indices_batching_dims=(0,),
)


def lane_lookup(table, index):
    return lax.gather(
        table,
        index[..., None],
        LANE_GATHER,
        slice_sizes=(1, 1),
        mode=lax.GatherScatterMode.PROMISE_IN_BOUNDS,
    )


def load_table(table_ref, rows):
    channels, bins = table_ref.shape
    table = table_ref[...].astype(jnp.float32)
    steps = (table * TABLE_STEPS).astype(jnp.int32)
    packed = []
    for ch in range(0, channels, 2):
        row = steps[ch : ch + 1, :] * FIELD + steps[ch + 1 : ch + 2, :]
        packed.append(
            [jnp.broadcast_to(row[:, c : c + LANES], (rows, LANES)) for c in range(0, bins, LANES)]
        )
    return packed


def table_lookup(chunks, bins):
    if len(chunks) == 1:
        both = lane_lookup(chunks[0], bins)
    else:
        low = bins % LANES
        high = bins // LANES
        both = lane_lookup(chunks[0], low)
        for c in range(1, len(chunks)):
            both = jnp.where(high == c, lane_lookup(chunks[c], low), both)
    first = lax.shift_right_logical(both, FIELD_BITS)
    second = both & (FIELD - 1)
    return first.astype(jnp.float32), second.astype(jnp.float32)


def block_partial(cells, packed, depth_cells, ray_step):
    rate_scale = -ray_step * math.log2(math.e) / TABLE_STEPS
    color = [None] * 3
    depth_sum = None
    for k in range(depth_cells):
        bright, bins = cells(k)
        bright = bright.astype(jnp.float32)
        red, green = table_lookup(packed[0], bins)
        blue, absorb = table_lookup(packed[1], bins)
        rate = bright * absorb
        if k:
            bright = bright * jnp.exp2(depth_sum * rate_scale)
        depth_sum = rate if depth_sum is None else depth_sum + rate
        for ch, factor in enumerate((red, green, blue)):
            term = bright * factor
            color[ch] = term if color[ch] is None else color[ch] + term
    scale = ray_step / TABLE_STEPS
    return [c * scale for c in color] + [jnp.exp2(depth_sum * rate_scale)]


def lookup(table, me):
    value = jnp.int32(table[0])
    for d in range(1, len(table)):
        value = jnp.where(me == d, jnp.int32(table[d]), value)
    return value


def write_piece(emis_ref, bins_ref, at, packed, out_ref, ray_step):
    depth_cells, piece_rows, cols = emis_ref.shape[-3:]
    for r in range(0, piece_rows, ROWS):
        for col in range(0, cols, LANES):

            def cells(k):
                block = (*at, k, slice(r, r + ROWS), slice(col, col + LANES))
                return emis_ref[block], bins_ref[block]

            planes = block_partial(cells, packed, depth_cells, ray_step)
            for ch, plane in enumerate(planes):
                out_ref[ch, r : r + ROWS, col : col + LANES] = plane


def first_kernel(
    emis_hbm, bins_hbm, table_hbm, order_hbm, *refs, targets, ray_step, ready
):
    n = len(targets)
    out_refs = refs[: n - 1]
    emis_own, bins_own, packed_ref, order_ref = refs[n - 1 : n + 3]
    emis_ref, bins_ref, table_ref, sems, table_sem, order_sem = refs[n + 3 :]
    me = lax.axis_index("depth")
    piece_rows = emis_own.shape[1]
    table_copy = pltpu.make_async_copy(table_hbm, table_ref, table_sem)
    table_copy.start()
    copies = []
    for s in range(n):
        row = pl.multiple_of(lookup(targets[s], me) * piece_rows, piece_rows)
        src = pl.ds(row, piece_rows)
        bins_to = bins_ref.at[s] if s < n - 1 else bins_own
        emis_to = emis_ref.at[s] if s < n - 1 else emis_own
        pair = (
            pltpu.make_async_copy(bins_hbm.at[:, src, :], bins_to, sems.at[s, 0]),
            pltpu.make_async_copy(emis_hbm.at[:, src, :], emis_to, sems.at[s, 1]),
        )
        copies.append(pair)
        for copy in pair:
            copy.start()
    order_copy = pltpu.make_async_copy(order_hbm, order_ref, order_sem)
    order_copy.start()
    table_copy.wait()
    packed = load_table(table_ref, ROWS)
    for pair, chunks in enumerate(packed):
        for c, chunk in enumerate(chunks):
            packed_ref[pair, c] = chunk
    start = 0
    for count in ready:
        some = range(start, min(start + count, n - 1))
        for s in some:
            for copy in copies[s]:
                copy.wait()
        for s in some:
            write_piece(emis_ref, bins_ref, (s,), packed, out_refs[s], ray_step)
        start += count
    for copy in copies[n - 1]:
        copy.wait()
    order_copy.wait()


def own_kernel(emis_ref, bins_ref, packed_ref, out_ref, *, ray_step):
    pairs, chunks = packed_ref.shape[:2]
    packed = [[packed_ref[pair, c] for c in range(chunks)] for pair in range(pairs)]
    write_piece(emis_ref, bins_ref, (), packed, out_ref, ray_step)


def composite_kernel(order_ref, *refs, slots):
    me = lax.axis_index("depth")
    in_refs, out_ref = refs[:-1], refs[-1]
    n = len(in_refs)

    def pick(slot, ch):
        value = in_refs[0][ch]
        for s in range(1, n):
            value = jnp.where(slot == s, in_refs[s][ch], value)
        return value

    flat = [s for row in slots for s in row]
    color = [None] * 3
    through = None
    for k in range(n):
        slot = lookup(flat, me * n + order_ref[k])
        for ch in range(3):
            term = pick(slot, ch)
            if k:
                term = color[ch] + through * term
            color[ch] = term
        passed = pick(slot, 3)
        through = passed if through is None else through * passed
    for ch in range(3):
        out_ref[ch] = color[ch]
    out_ref[3] = 1.0 - through


def assemble_kernel(*refs, sources):
    me = lax.axis_index("depth")
    in_refs, out_ref, sems = refs[:-2], refs[-2], refs[-1]
    piece_rows = in_refs[0].shape[1]
    copies = []
    for s, in_ref in enumerate(in_refs):
        row = pl.multiple_of(lookup(sources[s], me) * piece_rows, piece_rows)
        copies.append(
            pltpu.make_async_copy(in_ref, out_ref.at[:, pl.ds(row, piece_rows), :], sems.at[s])
        )
    for copy in copies:
        copy.start()
    for copy in copies:
        copy.wait()


def exchange(pieces, targets):
    received = []
    for s, target in enumerate(targets):
        received.append(lax.ppermute(pieces[s], "depth", list(enumerate(target))))
    return received


def rounds(devices, order):
    if devices == 4:
        return [list(target) for target in order]
    return [[d ^ s for d in range(devices)] for s in range(1, devices)]


def inverse(target):
    return [target.index(d) for d in range(len(target))]


VMEM = pl.BlockSpec(memory_space=pltpu.VMEM)
SMEM = pl.BlockSpec(memory_space=pltpu.SMEM)
ANY = pl.BlockSpec(memory_space=pl.ANY)


def in_vmem(arrays):
    return [pltpu.with_memory_space_constraint(a, pltpu.VMEM) for a in arrays]


def by_exchange(emissivity, bin_index, color_table, brick_order, devices, ray_step):
    depth_cells, cols_x, cols_y = emissivity.shape
    piece_rows = cols_x // devices
    out_targets = rounds(devices, OUT_ORDER)
    back_targets = rounds(devices, BACK_ORDER)
    mine_target = list(range(devices))
    piece = pltpu.VMEM((4, piece_rows, cols_y), jnp.float32)
    cells = (depth_cells, piece_rows, cols_y)
    n = devices
    channels, bins = color_table.shape
    *pieces, emis_own, bins_own, packed, order = pl.pallas_call(
        functools.partial(
            first_kernel, targets=out_targets + [mine_target], ray_step=ray_step, ready=READY if devices == 4 else (1,) * n
        ),
        out_shape=[piece] * (n - 1)
        + [
            pltpu.VMEM(cells, emissivity.dtype),
            pltpu.VMEM(cells, bin_index.dtype),
            pltpu.VMEM((channels // 2, bins // LANES, ROWS, LANES), jnp.int32),
            pltpu.SMEM(brick_order.shape, brick_order.dtype),
        ],
        in_specs=[ANY] * 4,
        out_specs=[VMEM] * (n + 2) + [SMEM],
        scratch_shapes=[
            pltpu.VMEM((n - 1, *cells), emissivity.dtype),
            pltpu.VMEM((n - 1, *cells), bin_index.dtype),
            pltpu.VMEM(color_table.shape, color_table.dtype),
            pltpu.SemaphoreType.DMA((n, 2)),
            pltpu.SemaphoreType.DMA,
            pltpu.SemaphoreType.DMA,
        ],
        name="first",
    )(emissivity, bin_index, color_table, brick_order)
    own = pl.pallas_call(
        functools.partial(own_kernel, ray_step=ray_step),
        out_shape=piece,
        in_specs=[VMEM] * 3,
        out_specs=VMEM,
        name="own_piece",
    )(*in_vmem([emis_own, bins_own, packed]))
    received = exchange(pieces, out_targets)
    slots = [[None] * devices for _ in range(devices)]
    for s, target in enumerate([mine_target] + out_targets):
        for d, t in enumerate(target):
            slots[t][d] = s
    mine = pl.pallas_call(
        functools.partial(composite_kernel, slots=slots),
        out_shape=pltpu.VMEM((4, piece_rows, cols_y), jnp.float32),
        in_specs=[SMEM] + [VMEM] * devices,
        out_specs=VMEM,
        name="composite",
    )(pltpu.with_memory_space_constraint(order, pltpu.SMEM), *in_vmem([own] + received))
    tiles = [mine] + exchange([mine] * (devices - 1), back_targets)
    sources = [inverse(t) for t in [mine_target] + back_targets]
    return pl.pallas_call(
        functools.partial(assemble_kernel, sources=sources),
        out_shape=jax.ShapeDtypeStruct((4, cols_x, cols_y), jnp.float32),
        in_specs=[VMEM] * devices,
        out_specs=ANY,
        scratch_shapes=[pltpu.SemaphoreType.DMA((devices,))],
        name="assemble",
    )(*in_vmem(tiles))


def whole_partial_kernel(emis_ref, bins_ref, table_ref, out_ref, *, ray_step, rows):
    packed = load_table(table_ref, rows)
    depth_cells, cols_x, cols_y = emis_ref.shape

    def step(b, carry):
        row = pl.multiple_of(b * rows, rows)
        for col in range(0, cols_y, LANES):

            def cells(k):
                at = (k, pl.ds(row, rows), slice(col, col + LANES))
                return emis_ref[at], bins_ref[at]

            planes = block_partial(cells, packed, depth_cells, ray_step)
            for ch, plane in enumerate(planes):
                out_ref[ch, pl.ds(row, rows), col : col + LANES] = plane
        return carry

    lax.fori_loop(0, cols_x // rows, step, 0)


def by_collectives(emissivity, bin_index, color_table, brick_order, devices, ray_step):
    _, cols_x, cols_y = emissivity.shape
    partials = pl.pallas_call(
        functools.partial(whole_partial_kernel, ray_step=ray_step, rows=8),
        out_shape=jax.ShapeDtypeStruct((4, cols_x, cols_y), jnp.float32),
        in_specs=[VMEM, VMEM, VMEM],
        out_specs=VMEM,
        name="partial_whole",
    )(emissivity, bin_index, color_table)
    pieces = partials.reshape(4, devices, cols_x // devices, cols_y).transpose(1, 0, 2, 3)
    received = lax.all_to_all(pieces, "depth", split_axis=0, concat_axis=0, tiled=True)

    def advance(state, brick):
        color, through = state
        planes = lax.dynamic_index_in_dim(received, brick, 0, keepdims=False)
        return (color + through * planes[0:3], through * planes[3]), None

    start = (jnp.zeros_like(received[0, 0:3]), jnp.ones_like(received[0, 3]))
    (color, through), _ = lax.scan(advance, start, brick_order)
    mine = jnp.concatenate([color, (1.0 - through)[None]], 0)
    return lax.all_gather(mine, "depth", axis=1, tiled=True)


def on_device(emissivity, bin_index, color_table, brick_order):
    depth_cells, cols_x, _ = emissivity.shape
    devices = lax.axis_size("depth")
    ray_step = 2.0 / (depth_cells * devices)
    few = devices in (2, 4, 8) and cols_x % (ROWS * devices) == 0
    plan = by_exchange if few else by_collectives
    return plan(emissivity, bin_index, color_table, brick_order, devices, ray_step)


def solution(mesh):
    return jax.shard_map(
        on_device,
        mesh=mesh,
        in_specs=(P("depth", "imgx", "imgy"), P("depth", "imgx", "imgy"), P(), P()),
        out_specs=P(None, "imgx", "imgy"),
        check_vma=False,
    )
```

profile of v0, /device:TPU:0, one launch (start us, length us, event | category | flops | bytes accessed | tf_op | source)
XLA Modules:
  0.0 22.1 jit_solution(10185661330680298383)
XLA Ops:
  0.0 1.7 %first.1 = (f32[4,32,128]{2,1,0:T(8,128)S(1)}, f32[4,32,128]{2,1,0:T(8,128)S(1)}, f32[4,32,128]{2,1,0:T(8,128)S(1)}, bf16[8,32,128]{2,1,0:T(8,128)(2,1)S(1)}, s3...) custom-call(bf16[8,128,128]{2,1,0:T(8,128)(2,1)} %emis_hbm.1, s32[8,128,128]{2,1,0:T(8,128)} %bins_hbm.1, ...), custom_call_target="tpu_custom_call" | custom-call | tf_op jit(solution)/shard_map/first/pallas_call | solution.py:238
  1.8 3.1 %collective-permute-start = (f32[4,32,128]{2,1,0:T(8,128)S(1)}, f32[4,32,128]{2,1,0:T(8,128)S(1)}, u32[]{:S(2)}, u32[]{:S(2)}) collective-permute-start(f32[4,32,128]{2,1,0:T(8,128)S(1)} %get-tuple-element.16), channel_id=1, source_target_pairs={{0,8},{8,24},{16,0},{24,16},{1,9},{9,25},{17,1},{25,17},{2,10},{10... | collective-permute-start | bytes 196616 | tf_op jit(solution)/shard_map/ppermute | solution.py:205
  4.9 2.5 %collective-permute-start.1 = (f32[4,32,128]{2,1,0:T(8,128)S(1)}, f32[4,32,128]{2,1,0:T(8,128)S(1)}, u32[]{:S(2)}, u32[]{:S(2)}) collective-permute-start(f32[4,32,128]{2,1,0:T(8,128)S(1)} %get-tuple-element.17), channel_id=1, source_target_pairs={{0,24},{8,16},{16,8},{24,0},{1,25},{9,17},{17,9},{25,1},{2,26},{10... | collective-permute-start | bytes 196616 | tf_op jit(solution)/shard_map/ppermute | solution.py:205
  7.3 1.6 %collective-permute-start.2 = (f32[4,32,128]{2,1,0:T(8,128)S(1)}, f32[4,32,128]{2,1,0:T(8,128)S(1)}, u32[]{:S(2)}, u32[]{:S(2)}) collective-permute-start(f32[4,32,128]{2,1,0:T(8,128)S(1)} %get-tuple-element.18), channel_id=1, source_target_pairs={{0,16},{8,0},{16,24},{24,8},{1,17},{9,1},{17,25},{25,9},{2,18},{10... | collective-permute-start | bytes 196616 | tf_op jit(solution)/shard_map/ppermute | solution.py:205
  8.9 0.2 %own_piece.1.refs_0_ = f32[4,32,128]{2,1,0:T(8,128)S(1)} custom-call(bf16[8,32,128]{2,1,0:T(8,128)(2,1)S(1)} %get-tuple-element.13.emis_ref, s32[8,32,128]{2,1,0:T(8,128)S(1)} %get-tuple-element.14.bins_ref, s32[2,1,8,128]{3,2,1,0:T(8,128)S(1)} %get-tuple-element.15.packed_ref), custom_call_target="tpu_custom_call" | custom-call | tf_op jit(solution)/shard_map/own_piece/pallas_call | solution.py:261
  9.1 0.0 collective-permute-done.refs_1_
  9.2 2.7 %collective-permute-done.1.refs_2_ = f32[4,32,128]{2,1,0:T(8,128)S(1)} collective-permute-done((f32[4,32,128]{2,1,0:T(8,128)S(1)}, f32[4,32,128]{2,1,0:T(8,128)S(1)}, u32[]{:S(2)}, u32[]{:S(2)}) %collective-permute-start.1) | collective-permute-done | bytes 65568 | tf_op jit(solution)/shard_map/ppermute | solution.py:205
  11.8 0.2 %collective-permute-done.2.refs_3_ = f32[4,32,128]{2,1,0:T(8,128)S(1)} collective-permute-done((f32[4,32,128]{2,1,0:T(8,128)S(1)}, f32[4,32,128]{2,1,0:T(8,128)S(1)}, u32[]{:S(2)}, u32[]{:S(2)}) %collective-permute-start.2) | collective-permute-done | bytes 65568 | tf_op jit(solution)/shard_map/ppermute | solution.py:205
  12.0 0.1 composite.1.refs_0_
  12.1 3.1 %collective-permute-start.5 = (f32[4,32,128]{2,1,0:T(8,128)S(1)}, f32[4,32,128]{2,1,0:T(8,128)S(1)}, u32[]{:S(2)}, u32[]{:S(2)}) collective-permute-start(f32[4,32,128]{2,1,0:T(8,128)S(1)} %composite.1.refs_0_), channel_id=1, source_target_pairs={{0,24},{8,0},{16,8},{24,16},{1,25},{9,1},{17,9},{25,17},{2,26},{10... | collective-permute-start | bytes 196616 | tf_op jit(solution)/shard_map/ppermute | solution.py:205
  15.3 0.0 collective-permute-start.4
  15.3 1.8 %collective-permute-start.3 = (f32[4,32,128]{2,1,0:T(8,128)S(1)}, f32[4,32,128]{2,1,0:T(8,128)S(1)}, u32[]{:S(2)}, u32[]{:S(2)}) collective-permute-start(f32[4,32,128]{2,1,0:T(8,128)S(1)} %composite.1.refs_0_), channel_id=1, source_target_pairs={{0,8},{8,16},{16,24},{24,0},{1,9},{9,17},{17,25},{25,1},{2,10},{10... | collective-permute-start | bytes 196616 | tf_op jit(solution)/shard_map/ppermute | solution.py:205
  17.1 0.1 collective-permute-done.5.refs_3_
  17.2 3.3 %collective-permute-done.4.refs_2_ = f32[4,32,128]{2,1,0:T(8,128)S(1)} collective-permute-done((f32[4,32,128]{2,1,0:T(8,128)S(1)}, f32[4,32,128]{2,1,0:T(8,128)S(1)}, u32[]{:S(2)}, u32[]{:S(2)}) %collective-permute-start.4) | collective-permute-done | bytes 65568 | tf_op jit(solution)/shard_map/ppermute | solution.py:205
  20.4 0.9 %collective-permute-done.3.refs_1_ = f32[4,32,128]{2,1,0:T(8,128)S(1)} collective-permute-done((f32[4,32,128]{2,1,0:T(8,128)S(1)}, f32[4,32,128]{2,1,0:T(8,128)S(1)}, u32[]{:S(2)}, u32[]{:S(2)}) %collective-permute-start.3) | collective-permute-done | bytes 65568 | tf_op jit(solution)/shard_map/ppermute | solution.py:205
  21.3 0.7 %assemble.1 = f32[4,128,128]{2,1,0:T(8,128)} custom-call(f32[4,32,128]{2,1,0:T(8,128)S(1)} %composite.1.refs_0_, f32[4,32,128]{2,1,0:T(8,128)S(1)} %collective-permute-done.3.refs_1_, f32[4,32,128]{2,1,0:T(8,128)S(1)} %collective-permute-done.4.refs_2_, f32[4,32,128]{2,1,0:T(8,128)S(1)} %collective-permute-done.5.refs_3_), custom_call_target="tpu_custom_call" | custom-call | tf_op jit(solution)/shard_map/assemble/pallas_call | solution.py:282
Async XLA Ops:
  1.8 7.4 %collective-permute-start = (f32[4,32,128]{2,1,0:T(8,128)S(1)}, f32[4,32,128]{2,1,0:T(8,128)S(1)}, u32[]{:S(2)}, u32[]{:S(2)}) collective-permute-start(f32[4,32,128]{2,1,0:T(8,128)S(1)} %get-tuple-element.16), channel_id=1, source_target_pairs={{0,8},{8,24},{16,0},{24,16},{1,9},{9,25},{17,1},{25,17},{2,10},{10... | collective-permute-start | bytes 196616 | tf_op jit(solution)/shard_map/ppermute | solution.py:205
  4.9 7.0 %collective-permute-start.1 = (f32[4,32,128]{2,1,0:T(8,128)S(1)}, f32[4,32,128]{2,1,0:T(8,128)S(1)}, u32[]{:S(2)}, u32[]{:S(2)}) collective-permute-start(f32[4,32,128]{2,1,0:T(8,128)S(1)} %get-tuple-element.17), channel_id=1, source_target_pairs={{0,24},{8,16},{16,8},{24,0},{1,25},{9,17},{17,9},{25,1},{2,26},{10... | collective-permute-start | bytes 196616 | tf_op jit(solution)/shard_map/ppermute | solution.py:205
  7.3 4.7 %collective-permute-start.2 = (f32[4,32,128]{2,1,0:T(8,128)S(1)}, f32[4,32,128]{2,1,0:T(8,128)S(1)}, u32[]{:S(2)}, u32[]{:S(2)}) collective-permute-start(f32[4,32,128]{2,1,0:T(8,128)S(1)} %get-tuple-element.18), channel_id=1, source_target_pairs={{0,16},{8,0},{16,24},{24,8},{1,17},{9,1},{17,25},{25,9},{2,18},{10... | collective-permute-start | bytes 196616 | tf_op jit(solution)/shard_map/ppermute | solution.py:205
  12.1 5.1 %collective-permute-start.5 = (f32[4,32,128]{2,1,0:T(8,128)S(1)}, f32[4,32,128]{2,1,0:T(8,128)S(1)}, u32[]{:S(2)}, u32[]{:S(2)}) collective-permute-start(f32[4,32,128]{2,1,0:T(8,128)S(1)} %composite.1.refs_0_), channel_id=1, source_target_pairs={{0,24},{8,0},{16,8},{24,16},{1,25},{9,1},{17,9},{25,17},{2,26},{10... | collective-permute-start | bytes 196616 | tf_op jit(solution)/shard_map/ppermute | solution.py:205
  15.3 5.2 %collective-permute-start.4 = (f32[4,32,128]{2,1,0:T(8,128)S(1)}, f32[4,32,128]{2,1,0:T(8,128)S(1)}, u32[]{:S(2)}, u32[]{:S(2)}) collective-permute-start(f32[4,32,128]{2,1,0:T(8,128)S(1)} %composite.1.refs_0_), channel_id=1, source_target_pairs={{0,16},{8,24},{16,0},{24,8},{1,17},{9,25},{17,1},{25,9},{2,18},{10... | collective-permute-start | bytes 196616 | tf_op jit(solution)/shard_map/ppermute | solution.py:205
  15.3 6.1 %collective-permute-start.3 = (f32[4,32,128]{2,1,0:T(8,128)S(1)}, f32[4,32,128]{2,1,0:T(8,128)S(1)}, u32[]{:S(2)}, u32[]{:S(2)}) collective-permute-start(f32[4,32,128]{2,1,0:T(8,128)S(1)} %composite.1.refs_0_), channel_id=1, source_target_pairs={{0,8},{8,16},{16,24},{24,0},{1,9},{9,17},{17,25},{25,1},{2,10},{10... | collective-permute-start | bytes 196616 | tf_op jit(solution)/shard_map/ppermute | solution.py:205
where the time goes:
time: 22.2 us; the launch traced here: 22.1 us
  starting transfers between devices  12.1 us (55%)
  waiting for transfers between devices  7.13 us (32%)
  Pallas kernels  2.77 us (12%)
    ppermute x6, starting transfers between devices, exchange(): received.append(lax.ppermute(pieces[s], 'depth', list(enumerate(target))))  12.1 us
    ppermute x6, waiting for transfers between devices, exchange(): received.append(lax.ppermute(pieces[s], 'depth', list(enumerate(target))))  7.13 us
    pallas_call x1, Pallas kernels, by_exchange(): pl.pallas_call(functools.partial(first_kernel, targets=out_targets + [min...  1.74 us
    pallas_call x1, Pallas kernels, by_exchange(): pl.pallas_call(functools.partial(assemble_kernel, sources=sources), out_s...  0.73 us
  transfers between devices with their start and end apart: 6, of which 5 were waited for; matrix products, arithmetic and copies ran while one was open for 0% of the time, Pallas kernels for 1%

commit v1 on v0

--- a/solution.py
+++ b/solution.py
@@ -14,7 +14,6 @@
 FIELD_BITS = 13
 FIELD = 1 << FIELD_BITS
 ROWS = 8
-READY = (3,)
 OUT_ORDER = ((1, 3, 0, 2), (3, 2, 1, 0), (2, 0, 3, 1))
 BACK_ORDER = ((1, 2, 3, 0), (2, 3, 0, 1), (3, 0, 1, 2))
 LANE_GATHER = lax.GatherDimensionNumbers(
@@ -105,28 +104,24 @@
 
 
 def first_kernel(
-    emis_hbm, bins_hbm, table_hbm, order_hbm, *refs, targets, ray_step, ready
+    emis_hbm, bins_hbm, table_hbm, order_hbm,
+    out_ref, second_ref, emis_rest, bins_rest, packed_ref, order_ref,
+    emis_first, bins_first, table_ref, sems, table_sem, order_sem,
+    *, targets, ray_step,
 ):
-    n = len(targets)
-    out_refs = refs[: n - 1]
-    emis_own, bins_own, packed_ref, order_ref = refs[n - 1 : n + 3]
-    emis_ref, bins_ref, table_ref, sems, table_sem, order_sem = refs[n + 3 :]
     me = lax.axis_index("depth")
-    piece_rows = emis_own.shape[1]
+    piece_rows = out_ref.shape[1]
     table_copy = pltpu.make_async_copy(table_hbm, table_ref, table_sem)
     table_copy.start()
     copies = []
-    for s in range(n):
+    for s in range(len(targets)):
         row = pl.multiple_of(lookup(targets[s], me) * piece_rows, piece_rows)
         src = pl.ds(row, piece_rows)
-        bins_to = bins_ref.at[s] if s < n - 1 else bins_own
-        emis_to = emis_ref.at[s] if s < n - 1 else emis_own
-        pair = (
-            pltpu.make_async_copy(bins_hbm.at[:, src, :], bins_to, sems.at[s, 0]),
-            pltpu.make_async_copy(emis_hbm.at[:, src, :], emis_to, sems.at[s, 1]),
-        )
-        copies.append(pair)
-        for copy in pair:
+        bins_to = bins_rest.at[s - 1] if s else bins_first
+        emis_to = emis_rest.at[s - 1] if s else emis_first
+        copies.append(pltpu.make_async_copy(bins_hbm.at[:, src, :], bins_to, sems.at[s, 0]))
+        copies.append(pltpu.make_async_copy(emis_hbm.at[:, src, :], emis_to, sems.at[s, 1]))
+        for copy in copies[-2:]:
             copy.start()
     order_copy = pltpu.make_async_copy(order_hbm, order_ref, order_sem)
     order_copy.start()
@@ -135,24 +130,22 @@
     for pair, chunks in enumerate(packed):
         for c, chunk in enumerate(chunks):
             packed_ref[pair, c] = chunk
-    start = 0
-    for count in ready:
-        some = range(start, min(start + count, n - 1))
-        for s in some:
-            for copy in copies[s]:
-                copy.wait()
-        for s in some:
-            write_piece(emis_ref, bins_ref, (s,), packed, out_refs[s], ray_step)
-        start += count
-    for copy in copies[n - 1]:
+    for copy in copies[:2]:
+        copy.wait()
+    write_piece(emis_first, bins_first, (), packed, out_ref, ray_step)
+    for copy in copies[2:4]:
+        copy.wait()
+    write_piece(emis_rest, bins_rest, (0,), packed, second_ref, ray_step)
+    for copy in copies[4:]:
         copy.wait()
     order_copy.wait()
 
 
-def own_kernel(emis_ref, bins_ref, packed_ref, out_ref, *, ray_step):
+def later_kernel(emis_ref, bins_ref, packed_ref, *out_refs, start, ray_step):
     pairs, chunks = packed_ref.shape[:2]
     packed = [[packed_ref[pair, c] for c in range(chunks)] for pair in range(pairs)]
-    write_piece(emis_ref, bins_ref, (), packed, out_ref, ray_step)
+    for s, out_ref in enumerate(out_refs):
+        write_piece(emis_ref, bins_ref, (start + s,), packed, out_ref, ray_step)
 
 
 def composite_kernel(order_ref, *refs, slots):
@@ -235,22 +228,21 @@
     cells = (depth_cells, piece_rows, cols_y)
     n = devices
     channels, bins = color_table.shape
-    *pieces, emis_own, bins_own, packed, order = pl.pallas_call(
-        functools.partial(
-            first_kernel, targets=out_targets + [mine_target], ray_step=ray_step, ready=READY if devices == 4 else (1,) * n
-        ),
-        out_shape=[piece] * (n - 1)
-        + [
-            pltpu.VMEM(cells, emissivity.dtype),
-            pltpu.VMEM(cells, bin_index.dtype),
+    first, second, emis_rest, bins_rest, packed, order = pl.pallas_call(
+        functools.partial(first_kernel, targets=out_targets + [mine_target], ray_step=ray_step),
+        out_shape=[
+            piece,
+            piece,
+            pltpu.VMEM((n - 1, *cells), emissivity.dtype),
+            pltpu.VMEM((n - 1, *cells), bin_index.dtype),
             pltpu.VMEM((channels // 2, bins // LANES, ROWS, LANES), jnp.int32),
             pltpu.SMEM(brick_order.shape, brick_order.dtype),
         ],
         in_specs=[ANY] * 4,
-        out_specs=[VMEM] * (n + 2) + [SMEM],
+        out_specs=[VMEM] * 5 + [SMEM],
         scratch_shapes=[
-            pltpu.VMEM((n - 1, *cells), emissivity.dtype),
-            pltpu.VMEM((n - 1, *cells), bin_index.dtype),
+            pltpu.VMEM(cells, emissivity.dtype),
+            pltpu.VMEM(cells, bin_index.dtype),
             pltpu.VMEM(color_table.shape, color_table.dtype),
             pltpu.SemaphoreType.DMA((n, 2)),
             pltpu.SemaphoreType.DMA,
@@ -258,13 +250,17 @@
         ],
         name="first",
     )(emissivity, bin_index, color_table, brick_order)
-    own = pl.pallas_call(
-        functools.partial(own_kernel, ray_step=ray_step),
-        out_shape=piece,
-        in_specs=[VMEM] * 3,
-        out_specs=VMEM,
-        name="own_piece",
-    )(*in_vmem([emis_own, bins_own, packed]))
+
+    def later(start, count):
+        return pl.pallas_call(
+            functools.partial(later_kernel, start=start, ray_step=ray_step),
+            out_shape=[piece] * count,
+            in_specs=[VMEM] * 3,
+            out_specs=[VMEM] * count,
+        )(*in_vmem([emis_rest, bins_rest, packed]))
+
+    pieces = [first, second] + list(later(1, n - 3))
+    (own,) = later(n - 2, 1)
     received = exchange(pieces, out_targets)
     slots = [[None] * devices for _ in range(devices)]
     for s, target in enumerate([mine_target] + out_targets):
@@ -336,7 +332,7 @@
     depth_cells, cols_x, _ = emissivity.shape
     devices = lax.axis_size("depth")
     ray_step = 2.0 / (depth_cells * devices)
-    few = devices in (2, 4, 8) and cols_x % (ROWS * devices) == 0
+    few = devices in (4, 8) and cols_x % (ROWS * devices) == 0
     plan = by_exchange if few else by_collectives
     return plan(emissivity, bin_index, color_table, brick_order, devices, ray_step)
 

time: 22.2 us -> 22.8 us (1.027)
  waiting for transfers between devices: 7.13 us -> 8.74 us
  starting transfers between devices: 12.1 us -> 11.1 us
    ppermute x6, waiting for transfers between devices: 7.13 us -> 8.74 us  [exchange(): received.append(lax.ppermute(pieces[s], 'depth', list(enumerate(target))))]
    ppermute x6, starting transfers between devices: 12.1 us -> 11.1 us  [exchange(): received.append(lax.ppermute(pieces[s], 'depth', list(enumerate(target))))]
    pallas_call x1 -> x2, Pallas kernels: 0.23 us -> 0.47 us  [later(): pl.pallas_call(functools.partial(later_kernel, start=start, ray_step=ray_...]
  transfers between devices with their start and end apart: 6 -> 6, of which waited for: 5 -> 4; matrix products, arithmetic and copies ran while one was open for 0% -> 0% of each run, Pallas kernels for 1% -> 1%
where the time goes in v1:
time: 22.8 us; the launch traced here: 22.7 us
  starting transfers between devices  11.1 us (49%)
  waiting for transfers between devices  8.74 us (38%)
  Pallas kernels  2.84 us (12%)
    ppermute x6, starting transfers between devices, exchange(): received.append(lax.ppermute(pieces[s], 'depth', list(enumerate(target))))  11.1 us
    ppermute x6, waiting for transfers between devices, exchange(): received.append(lax.ppermute(pieces[s], 'depth', list(enumerate(target))))  8.74 us
    pallas_call x1, Pallas kernels, by_exchange(): pl.pallas_call(functools.partial(first_kernel, targets=out_targets + [min...  1.58 us
    pallas_call x1, Pallas kernels, by_exchange(): pl.pallas_call(functools.partial(assemble_kernel, sources=sources), out_s...  0.73 us
    pallas_call x2, Pallas kernels, later(): pl.pallas_call(functools.partial(later_kernel, start=start, ray_step=ray_...  0.47 us
  transfers between devices with their start and end apart: 6, of which 4 were waited for; matrix products, arithmetic and copies ran while one was open for 0% of the time, Pallas kernels for 1%

profile of v1, /device:TPU:0, one launch (start us, length us, event | category | flops | bytes accessed | tf_op | source)
XLA Modules:
  0.0 22.7 jit_solution(12011196980263612175)
XLA Ops:
  0.0 1.6 %first.1 = (f32[4,32,128]{2,1,0:T(8,128)S(1)}, f32[4,32,128]{2,1,0:T(8,128)S(1)}, bf16[3,8,32,128]{3,2,1,0:T(8,128)(2,1)S(1)}, s32[3,8,32,128]{3,2,1,0:T(8,128)S...) custom-call(bf16[8,128,128]{2,1,0:T(8,128)(2,1)} %emis_hbm.1, s32[8,128,128]{2,1,0:T(8,128)} %bins_hbm.1, ...), custom_call_target="tpu_custom_call" | custom-call | tf_op jit(solution)/shard_map/first/pallas_call | solution.py:231
  1.6 0.2 %shard_map.47 = f32[4,32,128]{2,1,0:T(8,128)S(1)} custom-call(bf16[3,8,32,128]{3,2,1,0:T(8,128)(2,1)S(1)} %get-tuple-element.12.emis_ref, s32[3,8,32,128]{3,2,1,0:T(8,128)S(1)} %get-tuple-element.13.bins_ref, s32[2,1,8,128]{3,2,1,0:T(8,128)S(1)} %get-tuple-element.14.packed_ref), custom_call_target="tpu_custom_call" | custom-call | tf_op jit(solution)/shard_map/pallas_call | solution.py:255
  1.8 4.1 %collective-permute-start.2 = (f32[4,32,128]{2,1,0:T(8,128)S(1)}, f32[4,32,128]{2,1,0:T(8,128)S(1)}, u32[]{:S(2)}, u32[]{:S(2)}) collective-permute-start(f32[4,32,128]{2,1,0:T(8,128)S(1)} %shard_map.47), channel_id=1, source_target_pairs={{0,16},{8,0},{16,24},{24,8},{1,17},{9,1},{17,25},{25,9},{2,18},{10... | collective-permute-start | bytes 196616 | tf_op jit(solution)/shard_map/ppermute | solution.py:198
  5.9 0.0 collective-permute-start
  5.9 3.0 %collective-permute-start.1 = (f32[4,32,128]{2,1,0:T(8,128)S(1)}, f32[4,32,128]{2,1,0:T(8,128)S(1)}, u32[]{:S(2)}, u32[]{:S(2)}) collective-permute-start(f32[4,32,128]{2,1,0:T(8,128)S(1)} %get-tuple-element.16), channel_id=1, source_target_pairs={{0,24},{8,16},{16,8},{24,0},{1,25},{9,17},{17,9},{25,1},{2,26},{10... | collective-permute-start | bytes 196616 | tf_op jit(solution)/shard_map/ppermute | solution.py:198
  9.0 0.2 %shard_map.46.refs_0_ = f32[4,32,128]{2,1,0:T(8,128)S(1)} custom-call(bf16[3,8,32,128]{3,2,1,0:T(8,128)(2,1)S(1)} %get-tuple-element.12.emis_ref, s32[3,8,32,128]{3,2,1,0:T(8,128)S(1)} %get-tuple-element.13.bins_ref, s32[2,1,8,128]{3,2,1,0:T(8,128)S(1)} %get-tuple-element.14.packed_ref), custom_call_target="tpu_custom_call" | custom-call | tf_op jit(solution)/shard_map/pallas_call | solution.py:255
  9.2 0.0 collective-permute-done.2.refs_3_
  9.2 3.8 %collective-permute-done.refs_1_ = f32[4,32,128]{2,1,0:T(8,128)S(1)} collective-permute-done((f32[4,32,128]{2,1,0:T(8,128)S(1)}, f32[4,32,128]{2,1,0:T(8,128)S(1)}, u32[]{:S(2)}, u32[]{:S(2)}) %collective-permute-start) | collective-permute-done | bytes 65568 | tf_op jit(solution)/shard_map/ppermute | solution.py:198
  13.0 0.0 collective-permute-done.1.refs_2_
  13.0 0.1 composite.1.refs_0_
  13.1 2.2 %collective-permute-start.5 = (f32[4,32,128]{2,1,0:T(8,128)S(1)}, f32[4,32,128]{2,1,0:T(8,128)S(1)}, u32[]{:S(2)}, u32[]{:S(2)}) collective-permute-start(f32[4,32,128]{2,1,0:T(8,128)S(1)} %composite.1.refs_0_), channel_id=1, source_target_pairs={{0,24},{8,0},{16,8},{24,16},{1,25},{9,1},{17,9},{25,17},{2,26},{10... | collective-permute-start | bytes 196616 | tf_op jit(solution)/shard_map/ppermute | solution.py:198
  15.3 0.6 %collective-permute-start.4 = (f32[4,32,128]{2,1,0:T(8,128)S(1)}, f32[4,32,128]{2,1,0:T(8,128)S(1)}, u32[]{:S(2)}, u32[]{:S(2)}) collective-permute-start(f32[4,32,128]{2,1,0:T(8,128)S(1)} %composite.1.refs_0_), channel_id=1, source_target_pairs={{0,16},{8,24},{16,0},{24,8},{1,17},{9,25},{17,1},{25,9},{2,18},{10... | collective-permute-start | bytes 196616 | tf_op jit(solution)/shard_map/ppermute | solution.py:198
  15.9 1.1 %collective-permute-start.3 = (f32[4,32,128]{2,1,0:T(8,128)S(1)}, f32[4,32,128]{2,1,0:T(8,128)S(1)}, u32[]{:S(2)}, u32[]{:S(2)}) collective-permute-start(f32[4,32,128]{2,1,0:T(8,128)S(1)} %composite.1.refs_0_), channel_id=1, source_target_pairs={{0,8},{8,16},{16,24},{24,0},{1,9},{9,17},{17,25},{25,1},{2,10},{10... | collective-permute-start | bytes 196616 | tf_op jit(solution)/shard_map/ppermute | solution.py:198
  17.0 0.7 %collective-permute-done.5.refs_3_ = f32[4,32,128]{2,1,0:T(8,128)S(1)} collective-permute-done((f32[4,32,128]{2,1,0:T(8,128)S(1)}, f32[4,32,128]{2,1,0:T(8,128)S(1)}, u32[]{:S(2)}, u32[]{:S(2)}) %collective-permute-start.5) | collective-permute-done | bytes 65568 | tf_op jit(solution)/shard_map/ppermute | solution.py:198
  17.8 3.2 %collective-permute-done.4.refs_2_ = f32[4,32,128]{2,1,0:T(8,128)S(1)} collective-permute-done((f32[4,32,128]{2,1,0:T(8,128)S(1)}, f32[4,32,128]{2,1,0:T(8,128)S(1)}, u32[]{:S(2)}, u32[]{:S(2)}) %collective-permute-start.4) | collective-permute-done | bytes 65568 | tf_op jit(solution)/shard_map/ppermute | solution.py:198
  21.0 1.0 %collective-permute-done.3.refs_1_ = f32[4,32,128]{2,1,0:T(8,128)S(1)} collective-permute-done((f32[4,32,128]{2,1,0:T(8,128)S(1)}, f32[4,32,128]{2,1,0:T(8,128)S(1)}, u32[]{:S(2)}, u32[]{:S(2)}) %collective-permute-start.3) | collective-permute-done | bytes 65568 | tf_op jit(solution)/shard_map/ppermute | solution.py:198
  22.0 0.7 %assemble.1 = f32[4,128,128]{2,1,0:T(8,128)} custom-call(f32[4,32,128]{2,1,0:T(8,128)S(1)} %composite.1.refs_0_, f32[4,32,128]{2,1,0:T(8,128)S(1)} %collective-permute-done.3.refs_1_, f32[4,32,128]{2,1,0:T(8,128)S(1)} %collective-permute-done.4.refs_2_, f32[4,32,128]{2,1,0:T(8,128)S(1)} %collective-permute-done.5.refs_3_), custom_call_target="tpu_custom_call" | custom-call | tf_op jit(solution)/shard_map/assemble/pallas_call | solution.py:278
Async XLA Ops:
  1.8 7.4 %collective-permute-start.2 = (f32[4,32,128]{2,1,0:T(8,128)S(1)}, f32[4,32,128]{2,1,0:T(8,128)S(1)}, u32[]{:S(2)}, u32[]{:S(2)}) collective-permute-start(f32[4,32,128]{2,1,0:T(8,128)S(1)} %shard_map.47), channel_id=1, source_target_pairs={{0,16},{8,0},{16,24},{24,8},{1,17},{9,1},{17,25},{25,9},{2,18},{10... | collective-permute-start | bytes 196616 | tf_op jit(solution)/shard_map/ppermute | solution.py:198
  5.9 7.1 %collective-permute-start = (f32[4,32,128]{2,1,0:T(8,128)S(1)}, f32[4,32,128]{2,1,0:T(8,128)S(1)}, u32[]{:S(2)}, u32[]{:S(2)}) collective-permute-start(f32[4,32,128]{2,1,0:T(8,128)S(1)} %get-tuple-element.15), channel_id=1, source_target_pairs={{0,8},{8,24},{16,0},{24,16},{1,9},{9,25},{17,1},{25,17},{2,10},{10... | collective-permute-start | bytes 196616 | tf_op jit(solution)/shard_map/ppermute | solution.py:198
  5.9 7.1 %collective-permute-start.1 = (f32[4,32,128]{2,1,0:T(8,128)S(1)}, f32[4,32,128]{2,1,0:T(8,128)S(1)}, u32[]{:S(2)}, u32[]{:S(2)}) collective-permute-start(f32[4,32,128]{2,1,0:T(8,128)S(1)} %get-tuple-element.16), channel_id=1, source_target_pairs={{0,24},{8,16},{16,8},{24,0},{1,25},{9,17},{17,9},{25,1},{2,26},{10... | collective-permute-start | bytes 196616 | tf_op jit(solution)/shard_map/ppermute | solution.py:198
  13.1 4.7 %collective-permute-start.5 = (f32[4,32,128]{2,1,0:T(8,128)S(1)}, f32[4,32,128]{2,1,0:T(8,128)S(1)}, u32[]{:S(2)}, u32[]{:S(2)}) collective-permute-start(f32[4,32,128]{2,1,0:T(8,128)S(1)} %composite.1.refs_0_), channel_id=1, source_target_pairs={{0,24},{8,0},{16,8},{24,16},{1,25},{9,1},{17,9},{25,17},{2,26},{10... | collective-permute-start | bytes 196616 | tf_op jit(solution)/shard_map/ppermute | solution.py:198
  15.3 5.7 %collective-permute-start.4 = (f32[4,32,128]{2,1,0:T(8,128)S(1)}, f32[4,32,128]{2,1,0:T(8,128)S(1)}, u32[]{:S(2)}, u32[]{:S(2)}) collective-permute-start(f32[4,32,128]{2,1,0:T(8,128)S(1)} %composite.1.refs_0_), channel_id=1, source_target_pairs={{0,16},{8,24},{16,0},{24,8},{1,17},{9,25},{17,1},{25,9},{2,18},{10... | collective-permute-start | bytes 196616 | tf_op jit(solution)/shard_map/ppermute | solution.py:198
  15.9 6.1 %collective-permute-start.3 = (f32[4,32,128]{2,1,0:T(8,128)S(1)}, f32[4,32,128]{2,1,0:T(8,128)S(1)}, u32[]{:S(2)}, u32[]{:S(2)}) collective-permute-start(f32[4,32,128]{2,1,0:T(8,128)S(1)} %composite.1.refs_0_), channel_id=1, source_target_pairs={{0,8},{8,16},{16,24},{24,0},{1,9},{9,17},{17,25},{25,1},{2,10},{10... | collective-permute-start | bytes 196616 | tf_op jit(solution)/shard_map/ppermute | solution.py:198

commit v2 on v1

--- a/solution.py
+++ b/solution.py
@@ -178,7 +178,7 @@
 
 def assemble_kernel(*refs, sources):
     me = lax.axis_index("depth")
-    in_refs, out_ref, sems = refs[:-2], refs[-2], refs[-1]
+    in_refs, out_ref, sems = refs[: len(sources)], refs[-2], refs[-1]
     piece_rows = in_refs[0].shape[1]
     copies = []
     for s, in_ref in enumerate(in_refs):
@@ -275,14 +275,22 @@
     )(pltpu.with_memory_space_constraint(order, pltpu.SMEM), *in_vmem([own] + received))
     tiles = [mine] + exchange([mine] * (devices - 1), back_targets)
     sources = [inverse(t) for t in [mine_target] + back_targets]
-    return pl.pallas_call(
-        functools.partial(assemble_kernel, sources=sources),
-        out_shape=jax.ShapeDtypeStruct((4, cols_x, cols_y), jnp.float32),
-        in_specs=[VMEM] * devices,
-        out_specs=ANY,
-        scratch_shapes=[pltpu.SemaphoreType.DMA((devices,))],
-        name="assemble",
-    )(*in_vmem(tiles))
+    early = n // 2
+
+    def place(some, image):
+        given = [] if image is None else [image]
+        count = len(sources[some])
+        return pl.pallas_call(
+            functools.partial(assemble_kernel, sources=sources[some]),
+            out_shape=jax.ShapeDtypeStruct((4, cols_x, cols_y), jnp.float32),
+            in_specs=[VMEM] * count + [ANY] * len(given),
+            out_specs=ANY,
+            scratch_shapes=[pltpu.SemaphoreType.DMA((count,))],
+            input_output_aliases={count: 0} if given else {},
+        )(*in_vmem(tiles[some]), *given)
+
+    image = place(slice(0, early), None)
+    return place(slice(early, n), image)
 
 
 def whole_partial_kernel(emis_ref, bins_ref, table_ref, out_ref, *, ray_step, rows):

time: 22.8 us -> 23 us (level)
  Pallas kernels: 2.84 us -> 3.45 us
  waiting for transfers between devices: 8.74 us -> 8.25 us
    pallas_call x1 -> x2, Pallas kernels: 0.73 us -> 1.33 us  [place(): pl.pallas_call(functools.partial(assemble_kernel, sources=sources[some]),...]
    ppermute x6, waiting for transfers between devices: 8.74 us -> 8.25 us  [exchange(): received.append(lax.ppermute(pieces[s], 'depth', list(enumerate(target))))]
  transfers between devices with their start and end apart: 6 -> 6, of which waited for: 4 -> 3; matrix products, arithmetic and copies ran while one was open for 0% -> 0% of each run, Pallas kernels for 1% -> 4%
where the time goes in v2:
time: 23 us; the launch traced here: 22.8 us
  starting transfers between devices  11.1 us (48%)
  waiting for transfers between devices  8.25 us (36%)
  Pallas kernels  3.45 us (15%)
    ppermute x6, starting transfers between devices, exchange(): received.append(lax.ppermute(pieces[s], 'depth', list(enumerate(target))))  11.1 us
    ppermute x6, waiting for transfers between devices, exchange(): received.append(lax.ppermute(pieces[s], 'depth', list(enumerate(target))))  8.25 us
    pallas_call x1, Pallas kernels, by_exchange(): pl.pallas_call(functools.partial(first_kernel, targets=out_targets + [min...  1.58 us
    pallas_call x2, Pallas kernels, place(): pl.pallas_call(functools.partial(assemble_kernel, sources=sources[some]),...  1.33 us
    pallas_call x2, Pallas kernels, later(): pl.pallas_call(functools.partial(later_kernel, start=start, ray_step=ray_...  0.47 us
  transfers between devices with their start and end apart: 6, of which 3 were waited for; matrix products, arithmetic and copies ran while one was open for 0% of the time, Pallas kernels for 4%

profile of v2, /device:TPU:0, one launch (start us, length us, event | category | flops | bytes accessed | tf_op | source)
XLA Modules:
  0.0 22.8 jit_solution(436818306986351331)
XLA Ops:
  0.0 1.6 %first.1 = (f32[4,32,128]{2,1,0:T(8,128)S(1)}, f32[4,32,128]{2,1,0:T(8,128)S(1)}, bf16[3,8,32,128]{3,2,1,0:T(8,128)(2,1)S(1)}, s32[3,8,32,128]{3,2,1,0:T(8,128)S...) custom-call(bf16[8,128,128]{2,1,0:T(8,128)(2,1)} %emis_hbm.1, s32[8,128,128]{2,1,0:T(8,128)} %bins_hbm.1, ...), custom_call_target="tpu_custom_call" | custom-call | tf_op jit(solution)/shard_map/first/pallas_call | solution.py:231
  1.6 0.2 %shard_map.47 = f32[4,32,128]{2,1,0:T(8,128)S(1)} custom-call(bf16[3,8,32,128]{3,2,1,0:T(8,128)(2,1)S(1)} %get-tuple-element.12.emis_ref, s32[3,8,32,128]{3,2,1,0:T(8,128)S(1)} %get-tuple-element.13.bins_ref, s32[2,1,8,128]{3,2,1,0:T(8,128)S(1)} %get-tuple-element.14.packed_ref), custom_call_target="tpu_custom_call" | custom-call | tf_op jit(solution)/shard_map/pallas_call | solution.py:255
  1.8 4.1 %collective-permute-start.2 = (f32[4,32,128]{2,1,0:T(8,128)S(1)}, f32[4,32,128]{2,1,0:T(8,128)S(1)}, u32[]{:S(2)}, u32[]{:S(2)}) collective-permute-start(f32[4,32,128]{2,1,0:T(8,128)S(1)} %shard_map.47), channel_id=1, source_target_pairs={{0,16},{8,0},{16,24},{24,8},{1,17},{9,1},{17,25},{25,9},{2,18},{10... | collective-permute-start | bytes 196616 | tf_op jit(solution)/shard_map/ppermute | solution.py:198
  5.9 0.0 collective-permute-start
  5.9 3.0 %collective-permute-start.1 = (f32[4,32,128]{2,1,0:T(8,128)S(1)}, f32[4,32,128]{2,1,0:T(8,128)S(1)}, u32[]{:S(2)}, u32[]{:S(2)}) collective-permute-start(f32[4,32,128]{2,1,0:T(8,128)S(1)} %get-tuple-element.16), channel_id=1, source_target_pairs={{0,24},{8,16},{16,8},{24,0},{1,25},{9,17},{17,9},{25,1},{2,26},{10... | collective-permute-start | bytes 196616 | tf_op jit(solution)/shard_map/ppermute | solution.py:198
  9.0 0.2 %shard_map.46.refs_0_ = f32[4,32,128]{2,1,0:T(8,128)S(1)} custom-call(bf16[3,8,32,128]{3,2,1,0:T(8,128)(2,1)S(1)} %get-tuple-element.12.emis_ref, s32[3,8,32,128]{3,2,1,0:T(8,128)S(1)} %get-tuple-element.13.bins_ref, s32[2,1,8,128]{3,2,1,0:T(8,128)S(1)} %get-tuple-element.14.packed_ref), custom_call_target="tpu_custom_call" | custom-call | tf_op jit(solution)/shard_map/pallas_call | solution.py:255
  9.2 0.0 collective-permute-done.2.refs_3_
  9.2 3.8 %collective-permute-done.refs_1_ = f32[4,32,128]{2,1,0:T(8,128)S(1)} collective-permute-done((f32[4,32,128]{2,1,0:T(8,128)S(1)}, f32[4,32,128]{2,1,0:T(8,128)S(1)}, u32[]{:S(2)}, u32[]{:S(2)}) %collective-permute-start) | collective-permute-done | bytes 65568 | tf_op jit(solution)/shard_map/ppermute | solution.py:198
  13.0 0.0 collective-permute-done.1.refs_2_
  13.0 0.1 composite.1.refs_0_
  13.1 1.3 %collective-permute-start.5 = (f32[4,32,128]{2,1,0:T(8,128)S(1)}, f32[4,32,128]{2,1,0:T(8,128)S(1)}, u32[]{:S(2)}, u32[]{:S(2)}) collective-permute-start(f32[4,32,128]{2,1,0:T(8,128)S(1)} %composite.1.refs_0_), channel_id=1, source_target_pairs={{0,8},{8,16},{16,24},{24,0},{1,9},{9,17},{17,25},{25,1},{2,10},{10... | collective-permute-start | bytes 196616 | tf_op jit(solution)/shard_map/ppermute | solution.py:198
  14.4 2.6 %collective-permute-start.4 = (f32[4,32,128]{2,1,0:T(8,128)S(1)}, f32[4,32,128]{2,1,0:T(8,128)S(1)}, u32[]{:S(2)}, u32[]{:S(2)}) collective-permute-start(f32[4,32,128]{2,1,0:T(8,128)S(1)} %composite.1.refs_0_), channel_id=1, source_target_pairs={{0,24},{8,0},{16,8},{24,16},{1,25},{9,1},{17,9},{25,17},{2,26},{10... | collective-permute-start | bytes 196616 | tf_op jit(solution)/shard_map/ppermute | solution.py:198
  17.0 0.0 collective-permute-start.3
  17.0 2.4 %collective-permute-done.5.refs_1_ = f32[4,32,128]{2,1,0:T(8,128)S(1)} collective-permute-done((f32[4,32,128]{2,1,0:T(8,128)S(1)}, f32[4,32,128]{2,1,0:T(8,128)S(1)}, u32[]{:S(2)}, u32[]{:S(2)}) %collective-permute-start.5) | collective-permute-done | bytes 65568 | tf_op jit(solution)/shard_map/ppermute | solution.py:198
  19.5 0.7 %shard_map.48.refs_2_ = f32[4,128,128]{2,1,0:T(8,128)} custom-call(f32[4,32,128]{2,1,0:T(8,128)S(1)} %composite.1.refs_0_, f32[4,32,128]{2,1,0:T(8,128)S(1)} %collective-permute-done.5.refs_1_), custom_call_target="tpu_custom_call" | custom-call | tf_op jit(solution)/shard_map/pallas_call | solution.py:283
  20.1 0.0 collective-permute-done.4.refs_1_
  20.1 2.0 %collective-permute-done.3.refs_0_ = f32[4,32,128]{2,1,0:T(8,128)S(1)} collective-permute-done((f32[4,32,128]{2,1,0:T(8,128)S(1)}, f32[4,32,128]{2,1,0:T(8,128)S(1)}, u32[]{:S(2)}, u32[]{:S(2)}) %collective-permute-start.3) | collective-permute-done | bytes 65568 | tf_op jit(solution)/shard_map/ppermute | solution.py:198
  22.2 0.7 %shard_map.49 = f32[4,128,128]{2,1,0:T(8,128)} custom-call(f32[4,32,128]{2,1,0:T(8,128)S(1)} %collective-permute-done.3.refs_0_, f32[4,32,128]{2,1,0:T(8,128)S(1)} %collective-permute-done.4.refs_1_, f32[4,128,128]{2,1,0:T(8,128)} %shard_map.48.refs_2_), custom_call_target="tpu_custom_call", output_to_operand_aliasing={{}: (2, {})} | custom-call | tf_op jit(solution)/shard_map/pallas_call | solution.py:283
Async XLA Ops:
  1.8 7.4 %collective-permute-start.2 = (f32[4,32,128]{2,1,0:T(8,128)S(1)}, f32[4,32,128]{2,1,0:T(8,128)S(1)}, u32[]{:S(2)}, u32[]{:S(2)}) collective-permute-start(f32[4,32,128]{2,1,0:T(8,128)S(1)} %shard_map.47), channel_id=1, source_target_pairs={{0,16},{8,0},{16,24},{24,8},{1,17},{9,1},{17,25},{25,9},{2,18},{10... | collective-permute-start | bytes 196616 | tf_op jit(solution)/shard_map/ppermute | solution.py:198
  5.9 7.1 %collective-permute-start = (f32[4,32,128]{2,1,0:T(8,128)S(1)}, f32[4,32,128]{2,1,0:T(8,128)S(1)}, u32[]{:S(2)}, u32[]{:S(2)}) collective-permute-start(f32[4,32,128]{2,1,0:T(8,128)S(1)} %get-tuple-element.15), channel_id=1, source_target_pairs={{0,8},{8,24},{16,0},{24,16},{1,9},{9,25},{17,1},{25,17},{2,10},{10... | collective-permute-start | bytes 196616 | tf_op jit(solution)/shard_map/ppermute | solution.py:198
  5.9 7.1 %collective-permute-start.1 = (f32[4,32,128]{2,1,0:T(8,128)S(1)}, f32[4,32,128]{2,1,0:T(8,128)S(1)}, u32[]{:S(2)}, u32[]{:S(2)}) collective-permute-start(f32[4,32,128]{2,1,0:T(8,128)S(1)} %get-tuple-element.16), channel_id=1, source_target_pairs={{0,24},{8,16},{16,8},{24,0},{1,25},{9,17},{17,9},{25,1},{2,26},{10... | collective-permute-start | bytes 196616 | tf_op jit(solution)/shard_map/ppermute | solution.py:198
  13.1 6.3 %collective-permute-start.5 = (f32[4,32,128]{2,1,0:T(8,128)S(1)}, f32[4,32,128]{2,1,0:T(8,128)S(1)}, u32[]{:S(2)}, u32[]{:S(2)}) collective-permute-start(f32[4,32,128]{2,1,0:T(8,128)S(1)} %composite.1.refs_0_), channel_id=1, source_target_pairs={{0,8},{8,16},{16,24},{24,0},{1,9},{9,17},{17,25},{25,1},{2,10},{10... | collective-permute-start | bytes 196616 | tf_op jit(solution)/shard_map/ppermute | solution.py:198
  14.4 5.7 %collective-permute-start.4 = (f32[4,32,128]{2,1,0:T(8,128)S(1)}, f32[4,32,128]{2,1,0:T(8,128)S(1)}, u32[]{:S(2)}, u32[]{:S(2)}) collective-permute-start(f32[4,32,128]{2,1,0:T(8,128)S(1)} %composite.1.refs_0_), channel_id=1, source_target_pairs={{0,24},{8,0},{16,8},{24,16},{1,25},{9,1},{17,9},{25,17},{2,26},{10... | collective-permute-start | bytes 196616 | tf_op jit(solution)/shard_map/ppermute | solution.py:198
  17.0 5.2 %collective-permute-start.3 = (f32[4,32,128]{2,1,0:T(8,128)S(1)}, f32[4,32,128]{2,1,0:T(8,128)S(1)}, u32[]{:S(2)}, u32[]{:S(2)}) collective-permute-start(f32[4,32,128]{2,1,0:T(8,128)S(1)} %composite.1.refs_0_), channel_id=1, source_target_pairs={{0,16},{8,24},{16,0},{24,8},{1,17},{9,25},{17,1},{25,9},{2,18},{10... | collective-permute-start | bytes 196616 | tf_op jit(solution)/shard_map/ppermute | solution.py:198
